TPU v7x, 32 devices: a whole 2x2x4 slice. The times are simulated.
32 devices in a mesh: pb: 4 (over x, core), ka: 8 (over z, y).
Axes of the slice: x: 2, y: 2, z: 4, core: 2. Of those that a mesh axis runs over, the one named last changes fastest.
Arguments:
- queries: bfloat16 [4096, 1024], P(('pb', 'ka')), may hold values from -6 to 6
- key_rows: bfloat16 [4096, 128], P(('pb', 'ka')), may hold values from -6 to 6
- value_rows: bfloat16 [4096, 128], P(('pb', 'ka')), may hold values from -6 to 6
- forward_out: bfloat16 [4096, 1024], P(('pb', 'ka')), may hold values from -6 to 6
- out_grad: bfloat16 [4096, 1024], P(('pb', 'ka')), may hold values from -4 to 4
- logsumexp: float32 [8, 4096], P(None, ('pb', 'ka')), may hold values from 3 to 7
- position: int32 [4096], P(('pb', 'ka')), may hold values from 0 to 4095, as said below
- segment: int32 [4096], P(('pb', 'ka')), may hold values from 0 to 7, as said below
Outputs:
- query_grad: bfloat16 [4096, 1024], P(('pb', 'ka'))
- key_grad: bfloat16 [4096, 128], P(('pb', 'ka'))
- value_grad: bfloat16 [4096, 128], P(('pb', 'ka'))
Inputs may be any that keep to these rules, and one draw needn't show every extreme that they name: `position`: a permutation of 0 to 4095; each aligned run of 128 rows holds 128 consecutive positions in increasing order. `segment`: the document of the row's position; each document is a nonempty run of consecutive positions, numbered in the order of positions, 8 documents in all.
All inputs are finite; a program needn't handle non-finite values.
Results may differ from a plain program's by a relative error of at most 0.0051.
Values may be sent and summed in bfloat16 or wider, within the bound.
No kernel may reach another device: no remote copies, remote signals or barrier semaphores. Data moves between devices by JAX's collectives and lax.ppermute only.
A program may use at most 64 MiB of HBM per device.

v0:
```python
import jax
import jax.numpy as jnp
from jax import lax
from jax.sharding import PartitionSpec as P


def tile_terms(query_tile, grad_tile, lse_tile, delta_tile, key_tile, value_tile, visible):
    tile_rows = query_tile.shape[0]
    head_width = key_tile.shape[1]
    head_count = query_tile.shape[1] // head_width
    score_scale = head_width ** (-0.5)
    query_heads = query_tile.reshape(tile_rows, head_count, head_width)
    grad_heads = grad_tile.reshape(tile_rows, head_count, head_width)
    scores = (
        jnp.einsum("qhd,kd->hqk", query_heads, key_tile, preferred_element_type=jnp.float32)
        * score_scale
    )
    weights = jnp.where(visible[None], jnp.exp(scores - lse_tile[:, :, None]), 0.0)
    rounded = weights.astype(jnp.bfloat16)
    value_term = jnp.einsum("hqk,qhd->kd", rounded, grad_heads, preferred_element_type=jnp.float32)
    grad_scores = jnp.einsum(
        "qhd,kd->hqk", grad_heads, value_tile, preferred_element_type=jnp.float32
    )
    score_grads = (weights * (grad_scores - delta_tile[:, :, None])).astype(jnp.bfloat16)
    query_term = jnp.einsum(
        "hqk,kd->qhd", score_grads, key_tile, preferred_element_type=jnp.float32
    ).reshape(tile_rows, head_count * head_width)
    key_term = jnp.einsum(
        "hqk,qhd->kd", score_grads, query_heads, preferred_element_type=jnp.float32
    )
    return (query_term, key_term, value_term)


def all_grads(
    query_block,
    grad_block,
    lse_block,
    delta_block,
    query_place,
    query_doc,
    key_block,
    value_block,
    key_place,
    key_doc,
):
    query_total = query_block.shape[0]
    key_total = key_block.shape[0]
    head_width = key_block.shape[1]
    row_width = query_block.shape[1]
    query_step = min(512, query_total)
    key_step = min(256, key_total)

    def over_queries(query_index, loop_state):
        query_out, key_out, value_out = loop_state
        query_start = query_index * query_step
        query_tile = lax.dynamic_slice_in_dim(query_block, query_start, query_step, 0)
        grad_tile = lax.dynamic_slice_in_dim(grad_block, query_start, query_step, 0)
        lse_tile = lax.dynamic_slice_in_dim(lse_block, query_start, query_step, 1)
        delta_tile = lax.dynamic_slice_in_dim(delta_block, query_start, query_step, 1)
        place_tile = lax.dynamic_slice_in_dim(query_place, query_start, query_step, 0)
        doc_tile = lax.dynamic_slice_in_dim(query_doc, query_start, query_step, 0)

        def over_keys(key_index, inner_state):
            query_acc, key_out, value_out = inner_state
            key_start = key_index * key_step
            key_tile = lax.dynamic_slice_in_dim(key_block, key_start, key_step, 0)
            value_tile = lax.dynamic_slice_in_dim(value_block, key_start, key_step, 0)
            key_place_tile = lax.dynamic_slice_in_dim(key_place, key_start, key_step, 0)
            key_doc_tile = lax.dynamic_slice_in_dim(key_doc, key_start, key_step, 0)
            visible = (key_place_tile[None, :] <= place_tile[:, None]) & (
                key_doc_tile[None, :] == doc_tile[:, None]
            )
            operands = (query_tile, grad_tile, lse_tile, delta_tile, key_tile, value_tile, visible)
            query_term, key_term, value_term = tile_terms(*operands)
            key_slab = lax.dynamic_slice_in_dim(key_out, key_start, key_step, 0)
            key_out = lax.dynamic_update_slice_in_dim(key_out, key_slab + key_term, key_start, 0)
            value_slab = lax.dynamic_slice_in_dim(value_out, key_start, key_step, 0)
            value_out = lax.dynamic_update_slice_in_dim(
                value_out, value_slab + value_term, key_start, 0
            )
            return (query_acc + query_term, key_out, value_out)

        inner_start = (jnp.zeros((query_step, row_width), jnp.float32), key_out, value_out)
        query_acc, key_out, value_out = lax.fori_loop(
            0, key_total // key_step, over_keys, inner_start
        )
        query_out = lax.dynamic_update_slice_in_dim(query_out, query_acc, query_start, 0)
        return (query_out, key_out, value_out)

    starting = (
        jnp.zeros((query_total, row_width), jnp.float32),
        jnp.zeros((key_total, head_width), jnp.float32),
        jnp.zeros((key_total, head_width), jnp.float32),
    )
    return lax.fori_loop(0, query_total // query_step, over_queries, starting)


def body(queries, key_rows, value_rows, forward_out, out_grad, logsumexp, position, segment):
    head_width = key_rows.shape[1]
    head_count = queries.shape[1] // head_width
    local_rows = queries.shape[0]
    score_scale = head_width ** (-0.5)
    delta_rows = jnp.sum(
        (out_grad.astype(jnp.float32) * forward_out.astype(jnp.float32)).reshape(
            local_rows, head_count, head_width
        ),
        axis=2,
    ).T
    query_block, grad_block, query_place, query_doc = (
        lax.all_gather(queries, "ka", axis=0, tiled=True),
        lax.all_gather(out_grad, "ka", axis=0, tiled=True),
        lax.all_gather(position, "ka", axis=0, tiled=True),
        lax.all_gather(segment, "ka", axis=0, tiled=True),
    )
    lse_block, delta_block = (
        lax.all_gather(logsumexp, "ka", axis=1, tiled=True),
        lax.all_gather(delta_rows, "ka", axis=1, tiled=True),
    )
    key_block, value_block, key_place, key_doc = (
        lax.all_gather(key_rows, "pb", axis=0, tiled=True),
        lax.all_gather(value_rows, "pb", axis=0, tiled=True),
        lax.all_gather(position, "pb", axis=0, tiled=True),
        lax.all_gather(segment, "pb", axis=0, tiled=True),
    )
    query_sum, key_sum, value_sum = all_grads(
        query_block,
        grad_block,
        lse_block,
        delta_block,
        query_place,
        query_doc,
        key_block,
        value_block,
        key_place,
        key_doc,
    )
    query_grad = lax.psum_scatter(query_sum * score_scale, "ka", scatter_dimension=0, tiled=True)
    key_grad, value_grad = (
        lax.psum_scatter(key_sum * score_scale, "pb", scatter_dimension=0, tiled=True),
        lax.psum_scatter(value_sum, "pb", scatter_dimension=0, tiled=True),
    )
    return (
        query_grad.astype(jnp.bfloat16),
        key_grad.astype(jnp.bfloat16),
        value_grad.astype(jnp.bfloat16),
    )


def solution(mesh):
    placed = (
        P(("pb", "ka"), None),
        P(("pb", "ka"), None),
        P(("pb", "ka"), None),
        P(("pb", "ka"), None),
        P(("pb", "ka"), None),
        P(None, ("pb", "ka")),
        P(("pb", "ka")),
        P(("pb", "ka")),
    )
    return jax.shard_map(
        body,
        mesh=mesh,
        in_specs=placed,
        out_specs=(P(("pb", "ka"), None), P(("pb", "ka"), None), P(("pb", "ka"), None)),
        check_vma=False,
    )
```

profile of v0, /device:TPU:0, one launch (start us, length us, event | category | flops | bytes accessed | tf_op | source)
XLA Modules:
  0.0 322.1 jit_solution(15213432203039361931)
XLA Ops:
  7.3 0.7 all-gather.7.cloned.1.call-update
  8.0 0.7 all-gather.9.cloned.1.call-update
  8.7 1.1 multiply_bitcast_fusion
  9.9 0.2 reduce_sum.9
  10.2 33.8 %all_gather.35 = f32[8,1024]{0,1:T(8,128)S(1)} all-gather(f32[8,128]{0,1:T(8,128)S(1)} %bitcast.125), channel_id=1, replica_groups=mesh['pb'=4,'ka'=8] {'ka'}, dimensions={1}, use_global_device_ids=true | all-gather | bytes 36864 | tf_op jit(solution)/shard_map/all_gather | solution.py:117
  44.1 5.1 %all-gather.2 = s32[4,1,128]{2,1,0:T(1,128)S(1)} all-gather(s32[1,1,128]{2,1,0:T(1,128)S(1)} %bitcast.128), channel_id=1, replica_groups=mesh['pb'=4,'ka'=8] {'pb'}, dimensions={0}, use_global_device_ids=true | all-gather | bytes 2560 | tf_op jit(solution)/shard_map/all_gather | solution.py:122
  49.2 5.0 %all-gather.3 = s32[4,1,128]{2,1,0:T(1,128)S(1)} all-gather(s32[1,1,128]{2,1,0:T(1,128)S(1)} %bitcast.130), channel_id=1, replica_groups=mesh['pb'=4,'ka'=8] {'pb'}, dimensions={0}, use_global_device_ids=true | all-gather | bytes 2560 | tf_op jit(solution)/shard_map/all_gather | solution.py:123
  54.2 20.7 %all-gather = s32[8,1,128]{2,1,0:T(1,128)S(1)} all-gather(s32[1,1,128]{2,1,0:T(1,128)S(1)} %bitcast.129), channel_id=1, replica_groups=mesh['pb'=4,'ka'=8] {'ka'}, dimensions={0}, use_global_device_ids=true | all-gather | bytes 4608 | tf_op jit(solution)/shard_map/all_gather | solution.py:112
  75.0 16.3 %all-gather.1 = s32[8,1,128]{2,1,0:T(1,128)S(1)} all-gather(s32[1,1,128]{2,1,0:T(1,128)S(1)} %bitcast.131), channel_id=1, replica_groups=mesh['pb'=4,'ka'=8] {'ka'}, dimensions={0}, use_global_device_ids=true | all-gather | bytes 4608 | tf_op jit(solution)/shard_map/all_gather | solution.py:113
  91.3 31.1 %all_gather.34 = f32[8,1024]{1,0:T(8,128)S(1)} all-gather(f32[8,128]{1,0:T(8,128)S(1)} %copy-done.17), channel_id=1, replica_groups=mesh['pb'=4,'ka'=8] {'ka'}, dimensions={1}, use_global_device_ids=true | all-gather | bytes 36864 | tf_op jit(solution)/shard_map/all_gather | solution.py:116
  122.3 5.4 %all_gather.36 = bf16[512,128]{1,0:T(8,128)(2,1)S(1)} all-gather(bf16[128,128]{1,0:T(8,128)(2,1)S(1)} %copy-done.15), channel_id=1, replica_groups=mesh['pb'=4,'ka'=8] {'pb'}, dimensions={0}, use_global_device_ids=true | all-gather | bytes 163840 | tf_op jit(solution)/shard_map/all_gather | solution.py:120
  127.7 5.9 %all_gather.39 = bf16[512,128]{1,0:T(8,128)(2,1)} all-gather(bf16[128,128]{1,0:T(8,128)(2,1)S(1)} %copy-done.16), channel_id=1, replica_groups=mesh['pb'=4,'ka'=8] {'pb'}, dimensions={0}, use_global_device_ids=true | all-gather | bytes 163840 | tf_op jit(solution)/shard_map/all_gather | solution.py:121
  133.6 0.7 broadcast.67
  134.3 2.5 broadcast_in_dim.49.clone
  136.9 42.4 %while.52 = (s32[]{:T(128)}, f32[1024,1024]{1,0:T(8,128)}, f32[512,128]{1,0:T(8,128)}, f32[512,128]{1,0:T(8,128)S(1)}, s32[1024]{0:T(1024)S(1)}, /*index=5*/s32[...) while((s32[]{:T(128)}, f32[1024,1024]{1,0:T(8,128)}, ...), condition=%wide.region_4.5_spmd, body=%wide.region_1.4_spmd.sunk | while | flops 1354170368 | bytes 52825124 | solution.py:95
  136.9 0.6 copy-done.13
  137.6 0.6 constant_dynamic-slice_fusion.7
  138.3 2.8 constant_dynamic-slice_fusion.6
  141.0 11.9 %while.53 = (s32[]{:T(128)}, f32[512,1024]{0,1:T(8,128)S(1)}, f32[512,128]{1,0:T(8,128)}, f32[512,128]{1,0:T(8,128)S(1)}, bf16[512,128]{1,0:T(8,128)(2,1)S(1)}, ...) while((s32[]{:T(128)}, f32[512,1024]{0,1:T(8,128)S(1)}, ...), condition=%wide.region_3.3_spmd.clone, body=%wide.region_2.2_spmd.clone.sunk | while | flops 1354170368 | bytes 39578024 | solution.py:84
  141.2 0.2 compare_and_fusion.2
  141.4 0.7 fusion.79
  142.3 1.1 fusion.83
  143.5 1.6 fusion.80
  145.1 0.8 fusion.82
  145.9 0.5 fusion.81
  146.3 0.6 bitcast_add_fusion.2
  147.2 0.2 compare_and_fusion.2
  147.3 0.7 fusion.79
  148.2 1.1 fusion.83
  149.4 1.6 fusion.80
  151.0 0.8 fusion.82
  151.8 0.5 fusion.81
  152.3 0.6 bitcast_add_fusion.2
  152.9 1.9 copy.56
  154.8 3.2 constant_dynamic-update-slice_fusion.2
  158.1 0.5 copy-done.13
  158.8 0.6 constant_dynamic-slice_fusion.7
  159.4 2.8 constant_dynamic-slice_fusion.6
  162.2 11.9 %while.53 = (s32[]{:T(128)}, f32[512,1024]{0,1:T(8,128)S(1)}, f32[512,128]{1,0:T(8,128)}, f32[512,128]{1,0:T(8,128)S(1)}, bf16[512,128]{1,0:T(8,128)(2,1)S(1)}, ...) while((s32[]{:T(128)}, f32[512,1024]{0,1:T(8,128)S(1)}, ...), condition=%wide.region_3.3_spmd.clone, body=%wide.region_2.2_spmd.clone.sunk | while | flops 1354170368 | bytes 39578024 | solution.py:84
  162.4 0.2 compare_and_fusion.2
  162.6 0.7 fusion.79
  163.5 1.1 fusion.83
  164.6 1.6 fusion.80
  166.3 0.8 fusion.82
  167.0 0.5 fusion.81
  167.5 0.6 bitcast_add_fusion.2
  168.3 0.2 compare_and_fusion.2
  168.5 0.7 fusion.79
  169.4 1.1 fusion.83
  170.6 1.6 fusion.80
  172.2 0.8 fusion.82
  173.0 0.5 fusion.81
  173.5 0.6 bitcast_add_fusion.2
  174.1 1.9 copy.56
  176.0 3.2 %constant_dynamic-update-slice_fusion.2 = f32[1024,1024]{1,0:T(8,128)} fusion(f32[1024,1024]{1,0:T(8,128)} %get-tuple-element.913, f32[512,1024]{1,0:T(8,128)} %copy.56, s32[]{:T(128)S(6)} %select_n.53), kind=kLoop, calls=%fused_computation.38.clone.1 | loop fusion | bytes 4194308 | tf_op jit(solution)/shard_map/while/body/eval_jaxpr/dynamic_update_slice | solution.py:87
  179.3 0.7 copy-done.1
  180.1 1.7 broadcast_multiply_fusion.1
  181.8 5.1 %broadcast_multiply_fusion = f32[1024,1024]{1,0:T(8,128)} fusion(f32[1024,1024]{1,0:T(8,128)} %get-tuple-element.501), kind=kLoop, calls=%fused_computation.43 | loop fusion | flops 1048576 | bytes 8388608 | tf_op jit(solution)/shard_map/mul | solution.py:137
  186.9 12.1 %reduce-scatter.8.cloned.1.call-done = f32[128,128]{1,0:T(8,128)} async-done(((f32[512,128]{1,0:T(8,128)}), f32[128,128]{1,0:T(8,128)}) %reduce-scatter.8.cloned.1.call-update) | async-done | bytes 65552 | tf_op jit(solution)/shard_map/reduce_scatter | solution.py:140
  199.0 1.5 convert_element_type.33
  200.5 21.5 %reduce-scatter.6.cloned.1.call-done = f32[128,128]{1,0:T(8,128)} async-done(((f32[512,128]{1,0:T(8,128)}), f32[128,128]{1,0:T(8,128)}) %reduce-scatter.6.cloned.1.call-update) | async-done | bytes 65552 | tf_op jit(solution)/shard_map/reduce_scatter | solution.py:139
  222.0 1.5 convert_element_type.32
  223.4 90.3 %reduce-scatter.4.cloned.1.call-done = f32[128,1024]{1,0:T(8,128)} async-done(((f32[1024,1024]{1,0:T(8,128)}), f32[128,1024]{1,0:T(8,128)}) %reduce-scatter.4.cloned.1.call-update) | async-done | bytes 524304 | tf_op jit(solution)/shard_map/reduce_scatter | solution.py:137
  313.8 1.8 convert_element_type.31
  (116 shorter events, 2.2 us)
Async XLA Ops:
  7.2 36.9 %copy-start.18 = (s32[128]{0:T(128)S(1)}, s32[128]{0:T(128)}, u32[]{:S(2)}) copy-start(s32[128]{0:T(128)} %param.18) | copy-start | bytes 1540
  7.2 42.0 %copy-start.19 = (s32[128]{0:T(128)S(1)}, s32[128]{0:T(128)}, u32[]{:S(2)}) copy-start(s32[128]{0:T(128)} %param.19) | copy-start | bytes 1540
  7.2 84.1 %copy-start.17 = (f32[8,128]{1,0:T(8,128)S(1)}, f32[8,128]{1,0:T(8,128)}, u32[]{:S(2)}) copy-start(f32[8,128]{1,0:T(8,128)} %param.17) | copy-start | bytes 12292
  7.2 115.1 %copy-start.15 = (bf16[128,128]{1,0:T(8,128)(2,1)S(1)}, bf16[128,128]{1,0:T(8,128)(2,1)}, u32[]{:S(2)}) copy-start(bf16[128,128]{1,0:T(8,128)(2,1)} %param.13) | copy-start | bytes 98308
  7.2 120.5 %copy-start.16 = (bf16[128,128]{1,0:T(8,128)(2,1)S(1)}, bf16[128,128]{1,0:T(8,128)(2,1)}, u32[]{:S(2)}) copy-start(bf16[128,128]{1,0:T(8,128)(2,1)} %param.14) | copy-start | bytes 98308
  7.2 126.4 %all-gather.7.cloned.1.call-start = ((), (), s32[]{:S(2)}) async-start(), calls=%async_computation.3 | async-start | bytes 2359296 | tf_op jit(solution)/shard_map/all_gather | solution.py:110
  8.0 125.6 %all-gather.9.cloned.1.call-start = ((), (), s32[]{:S(2)}) async-start(), calls=%async_computation.4 | async-start | bytes 2359296 | tf_op jit(solution)/shard_map/all_gather | solution.py:111
  8.7 190.3 %reduce-scatter.8.cloned.1.call-start = ((), (), s32[]{:S(2)}) async-start(), calls=%async_computation.7 | async-start | bytes 327680 | tf_op jit(solution)/shard_map/reduce_scatter | solution.py:140
  136.9 0.6 copy-start.13
  136.9 1.3 copy-start.6
  136.9 1.3 copy-start.8
  136.9 1.3 copy-start.11
  141.0 1.2 copy-start
  141.0 1.2 copy-start.5
  142.3 1.2 copy-start.4
  142.3 1.2 copy-start.10
  143.4 1.6 copy-start.2
  145.8 1.1 copy-start.3
  147.0 1.2 copy-start
  147.0 1.2 copy-start.5
  148.2 1.2 copy-start.4
  148.2 1.2 copy-start.10
  149.4 1.6 copy-start.2
  151.8 1.1 copy-start.3
  152.9 5.1 %copy-start.14 = (s32[1024]{0:T(1024)S(1)}, s32[1024]{0:T(1024)}, u32[]{:S(2)}) copy-start(s32[1024]{0:T(1024)} %copy-done.13) | copy-start | bytes 12292 | tf_op jit(solution)/shard_map/while
  154.8 3.2 copy-start.7
  154.8 3.2 copy-start.9
  154.8 3.2 copy-start.12
  158.1 0.6 copy-start.13
  158.1 1.3 copy-start.6
  158.1 1.3 copy-start.8
  158.1 1.3 copy-start.11
  162.2 1.2 copy-start
  162.2 1.2 copy-start.5
  163.4 1.2 copy-start.4
  163.5 1.2 copy-start.10
  164.6 1.6 copy-start.2
  167.0 1.1 copy-start.3
  168.2 1.2 copy-start
  168.2 1.2 copy-start.5
  169.4 1.2 copy-start.4
  169.4 1.2 copy-start.10
  170.6 1.6 copy-start.2
  173.0 1.1 copy-start.3
  174.1 5.2 %copy-start.14 = (s32[1024]{0:T(1024)S(1)}, s32[1024]{0:T(1024)}, u32[]{:S(2)}) copy-start(s32[1024]{0:T(1024)} %copy-done.13) | copy-start | bytes 12292 | tf_op jit(solution)/shard_map/while
  176.0 3.3 %copy-start.7 = (f32[8,1024]{1,0:T(8,128)S(1)}, f32[8,1024]{1,0:T(8,128)}, u32[]{:S(2)}) copy-start(f32[8,1024]{1,0:T(8,128)} %copy-done.6) | copy-start | bytes 98308 | tf_op jit(solution)/shard_map/while
  176.0 3.3 %copy-start.9 = (f32[8,1024]{1,0:T(8,128)S(1)}, f32[8,1024]{1,0:T(8,128)}, u32[]{:S(2)}) copy-start(f32[8,1024]{1,0:T(8,128)} %copy-done.8) | copy-start | bytes 98308 | tf_op jit(solution)/shard_map/while
  176.0 3.3 %copy-start.12 = (s32[1024]{0:T(1024)S(1)}, s32[1024]{0:T(1024)}, u32[]{:S(2)}) copy-start(s32[1024]{0:T(1024)} %copy-done.11) | copy-start | bytes 12292 | tf_op jit(solution)/shard_map/while
  179.3 0.7 copy-start.1
  180.0 41.9 %reduce-scatter.6.cloned.1.call-start = ((), (), s32[]{:S(2)}) async-start(), calls=%async_computation.6 | async-start | bytes 327680 | tf_op jit(solution)/shard_map/reduce_scatter | solution.py:139
  181.8 132.0 %reduce-scatter.4.cloned.1.call-start = ((), (), s32[]{:S(2)}) async-start(), calls=%async_computation.5 | async-start | bytes 4718592 | tf_op jit(solution)/shard_map/reduce_scatter | solution.py:137
Sparse Core Ops, SparseCore 0:
  10.2 53.5 all-gather.6
  65.9 48.1 all-gather.8
  180.1 18.8 reduce-scatter.7
  201.9 20.0 reduce-scatter.5
  225.4 88.2 reduce-scatter.3
where the time goes:
time: 323 us; the launch traced here: 322 us
  waiting for transfers between devices  125 us (39%)
  blocking collectives  123 us (38%)
  local copies, waits for them, and re-layouts  24.1 us (7%)
  matrix products  18.8 us (6%)
  other arithmetic  15.9 us (5%)
  between operations  13.9 us (4%)
    reduce_scatter x1, waiting for transfers between devices, body(): lax.psum_scatter(query_sum * score_scale, 'ka', scatter_dimension=0, tile...  90.3 us
    all_gather x1, blocking collectives, body(): lax.all_gather(delta_rows, 'ka', axis=1, tiled=True)  33.8 us
    all_gather x1, blocking collectives, body(): lax.all_gather(logsumexp, 'ka', axis=1, tiled=True)  31.1 us
    reduce_scatter x1, waiting for transfers between devices, body(): lax.psum_scatter(key_sum * score_scale, 'pb', scatter_dimension=0, tiled=...  21.5 us
    all_gather x1, blocking collectives, body(): lax.all_gather(position, 'ka', axis=0, tiled=True)  20.7 us
    all_gather x1, blocking collectives, body(): lax.all_gather(segment, 'ka', axis=0, tiled=True)  16.3 us
    reduce_scatter x1, waiting for transfers between devices, body(): lax.psum_scatter(value_sum, 'pb', scatter_dimension=0, tiled=True)  12.1 us
    dynamic_update_slice x4, local copies, waits for them, and re-layouts, over_queries(): lax.dynamic_update_slice_in_dim(query_out, query_acc, query_start, 0)  10.2 us
  transfers between devices with their start and end apart: 5, of which 3 were waited for; matrix products, arithmetic and copies ran while one was open for 3% of the time, Pallas kernels for 0%

commit v1 on v0

--- a/solution.py
+++ b/solution.py
@@ -2,6 +2,18 @@
 import jax.numpy as jnp
 from jax import lax
 from jax.sharding import PartitionSpec as P
+
+
+def doubled_up(array, axis, dim):
+    ways, here = (lax.axis_size(axis), lax.axis_index(axis))
+    grown, reach = (array, 1)
+    while reach < ways:
+        theirs = lax.ppermute(grown, axis, [(d, d ^ reach) for d in range(ways)])
+        mine_first = jnp.concatenate([grown, theirs], axis=dim)
+        theirs_first = jnp.concatenate([theirs, grown], axis=dim)
+        grown = jnp.where(here & reach == 0, mine_first, theirs_first)
+        reach = 2 * reach
+    return grown
 
 
 def tile_terms(query_tile, grad_tile, lse_tile, delta_tile, key_tile, value_tile, visible):
@@ -113,7 +125,7 @@
         lax.all_gather(segment, "ka", axis=0, tiled=True),
     )
     lse_block, delta_block = (
-        lax.all_gather(logsumexp, "ka", axis=1, tiled=True),
+        doubled_up(logsumexp, "ka", 1),
         lax.all_gather(delta_rows, "ka", axis=1, tiled=True),
     )
     key_block, value_block, key_place, key_doc = (

time: 323 us -> 307 us (0.950)
  blocking collectives: 123 us -> 90.1 us
  waiting for transfers between devices: 125 us -> 135 us
  starting transfers between devices: 0.2 us -> 7.49 us
    all_gather x1 -> x0, blocking collectives: 31.1 us -> none  [body(): lax.all_gather(logsumexp, 'ka', axis=1, tiled=True)]
    all_gather x1, waiting for transfers between devices: 0.01 us -> 9.54 us  [body(): lax.all_gather(out_grad, 'ka', axis=0, tiled=True)]
    ppermute x0 -> x3, starting transfers between devices: none -> 7.29 us  [doubled_up(): theirs = lax.ppermute(grown, axis, [(d, d ^ reach) for d in range(ways)])]
    all_gather x1, blocking collectives: 20.7 us -> 17 us  [body(): lax.all_gather(position, 'ka', axis=0, tiled=True)]
  transfers between devices with their start and end apart: 5 -> 8, of which waited for: 3 -> 4; matrix products, arithmetic and copies ran while one was open for 3% -> 4% of each run, Pallas kernels for 0% -> 0%
where the time goes in v1:
time: 307 us; the launch traced here: 306 us
  waiting for transfers between devices  135 us (44%)
  blocking collectives  90.1 us (29%)
  local copies, waits for them, and re-layouts  24.1 us (8%)
  matrix products  18.8 us (6%)
  other arithmetic  16.7 us (5%)
  between operations  13.9 us (5%)
  starting transfers between devices  7.49 us (2%)
    reduce_scatter x1, waiting for transfers between devices, body(): lax.psum_scatter(query_sum * score_scale, 'ka', scatter_dimension=0, tile...  90.4 us
    all_gather x1, blocking collectives, body(): lax.all_gather(delta_rows, 'ka', axis=1, tiled=True)  32.6 us
    reduce_scatter x1, waiting for transfers between devices, body(): lax.psum_scatter(key_sum * score_scale, 'pb', scatter_dimension=0, tiled=...  21.5 us
    all_gather x1, blocking collectives, body(): lax.all_gather(segment, 'ka', axis=0, tiled=True)  17.9 us
    all_gather x1, blocking collectives, body(): lax.all_gather(position, 'ka', axis=0, tiled=True)  17 us
    reduce_scatter x1, waiting for transfers between devices, body(): lax.psum_scatter(value_sum, 'pb', scatter_dimension=0, tiled=True)  11.8 us
    dynamic_update_slice x4, local copies, waits for them, and re-layouts, over_queries(): lax.dynamic_update_slice_in_dim(query_out, query_acc, query_start, 0)  10.2 us
    all_gather x1, waiting for transfers between devices, body(): lax.all_gather(out_grad, 'ka', axis=0, tiled=True)  9.54 us
  transfers between devices with their start and end apart: 8, of which 4 were waited for; matrix products, arithmetic and copies ran while one was open for 4% of the time, Pallas kernels for 0%

profile of v1, /device:TPU:0, one launch (start us, length us, event | category | flops | bytes accessed | tf_op | source)
XLA Modules:
  0.0 306.4 jit_solution(12599970486847328840)
XLA Ops:
  7.2 0.7 all-gather.7.cloned.1.call-update
  8.0 0.7 all-gather.9.cloned.1.call-update
  8.7 3.1 collective-permute-start
  11.8 1.1 multiply_bitcast_fusion
  12.9 5.6 %all_gather.32 = bf16[512,128]{1,0:T(8,128)(2,1)S(1)} all-gather(bf16[128,128]{1,0:T(8,128)(2,1)} %param.13), channel_id=1, replica_groups=mesh['pb'=4,'ka'=8] {'pb'}, dimensions={0}, use_global_device_ids=true | all-gather | bytes 163840 | tf_op jit(solution)/shard_map/all_gather | solution.py:132
  18.5 0.8 maximum_select_fusion.2
  19.3 1.6 collective-permute-start.1
  20.8 6.9 %all_gather.35 = bf16[512,128]{1,0:T(8,128)(2,1)} all-gather(bf16[128,128]{1,0:T(8,128)(2,1)} %param.14), channel_id=1, replica_groups=mesh['pb'=4,'ka'=8] {'pb'}, dimensions={0}, use_global_device_ids=true | all-gather | bytes 163840 | tf_op jit(solution)/shard_map/all_gather | solution.py:133
  27.8 0.2 reduce_sum.9
  28.1 2.7 collective-permute-start.2
  30.7 32.6 %all_gather.31 = f32[8,1024]{0,1:T(8,128)S(1)} all-gather(f32[8,128]{0,1:T(8,128)S(1)} %bitcast.125), channel_id=1, replica_groups=mesh['pb'=4,'ka'=8] {'ka'}, dimensions={1}, use_global_device_ids=true | all-gather | bytes 36864 | tf_op jit(solution)/shard_map/all_gather | solution.py:129
  63.5 5.1 %all-gather.2 = s32[4,1,128]{2,1,0:T(1,128)S(1)} all-gather(s32[1,1,128]{2,1,0:T(1,128)S(1)} %bitcast.128), channel_id=1, replica_groups=mesh['pb'=4,'ka'=8] {'pb'}, dimensions={0}, use_global_device_ids=true | all-gather | bytes 2560 | tf_op jit(solution)/shard_map/all_gather | solution.py:134
  68.5 5.0 %all-gather.3 = s32[4,1,128]{2,1,0:T(1,128)S(1)} all-gather(s32[1,1,128]{2,1,0:T(1,128)S(1)} %bitcast.130), channel_id=1, replica_groups=mesh['pb'=4,'ka'=8] {'pb'}, dimensions={0}, use_global_device_ids=true | all-gather | bytes 2560 | tf_op jit(solution)/shard_map/all_gather | solution.py:135
  73.6 17.0 %all-gather = s32[8,1,128]{2,1,0:T(1,128)S(1)} all-gather(s32[1,1,128]{2,1,0:T(1,128)S(1)} %bitcast.129), channel_id=1, replica_groups=mesh['pb'=4,'ka'=8] {'ka'}, dimensions={0}, use_global_device_ids=true | all-gather | bytes 4608 | tf_op jit(solution)/shard_map/all_gather | solution.py:124
  90.6 17.9 %all-gather.1 = s32[8,1,128]{2,1,0:T(1,128)S(1)} all-gather(s32[1,1,128]{2,1,0:T(1,128)S(1)} %bitcast.131), channel_id=1, replica_groups=mesh['pb'=4,'ka'=8] {'ka'}, dimensions={0}, use_global_device_ids=true | all-gather | bytes 4608 | tf_op jit(solution)/shard_map/all_gather | solution.py:125
  108.5 9.5 %all-gather.9.cloned.1.call-done = bf16[1024,1024]{1,0:T(8,128)(2,1)} async-done(((bf16[128,1024]{1,0:T(8,128)(2,1)}), bf16[1024,1024]{1,0:T(8,128)(2,1)}) %all-gather.9.cloned.1.call-update) | async-done | bytes 2097168 | tf_op jit(solution)/shard_map/all_gather | solution.py:123
  118.1 0.7 broadcast.67
  118.8 2.5 broadcast_in_dim.49.clone
  121.4 42.4 %while.52 = (s32[]{:T(128)}, f32[1024,1024]{1,0:T(8,128)}, f32[512,128]{1,0:T(8,128)}, f32[512,128]{1,0:T(8,128)S(1)}, s32[1024]{0:T(1024)S(1)}, /*index=5*/s32[...) while((s32[]{:T(128)}, f32[1024,1024]{1,0:T(8,128)}, ...), condition=%wide.region_4.5_spmd, body=%wide.region_1.4_spmd.sunk | while | flops 1354170368 | bytes 52825124 | solution.py:107
  121.4 0.6 copy-done.13
  122.1 0.6 constant_dynamic-slice_fusion.7
  122.7 2.8 constant_dynamic-slice_fusion.6
  125.5 11.9 %while.53 = (s32[]{:T(128)}, f32[512,1024]{0,1:T(8,128)S(1)}, f32[512,128]{1,0:T(8,128)}, f32[512,128]{1,0:T(8,128)S(1)}, bf16[512,128]{1,0:T(8,128)(2,1)S(1)}, ...) while((s32[]{:T(128)}, f32[512,1024]{0,1:T(8,128)S(1)}, ...), condition=%wide.region_3.3_spmd.clone, body=%wide.region_2.2_spmd.clone.sunk | while | flops 1354170368 | bytes 39578024 | solution.py:96
  125.9 0.7 fusion.79
  126.8 1.1 fusion.83
  127.9 1.6 fusion.80
  129.6 0.8 fusion.82
  130.3 0.5 fusion.81
  130.8 0.6 bitcast_add_fusion.2
  131.8 0.7 fusion.79
  132.7 1.1 fusion.83
  133.9 1.6 fusion.80
  135.5 0.8 fusion.82
  136.3 0.5 fusion.81
  136.8 0.6 bitcast_add_fusion.2
  137.4 1.9 copy.56
  139.3 3.2 %constant_dynamic-update-slice_fusion.2 = f32[1024,1024]{1,0:T(8,128)} fusion(f32[1024,1024]{1,0:T(8,128)} %get-tuple-element.913, f32[512,1024]{1,0:T(8,128)} %copy.56, s32[]{:T(128)S(6)} %select_n.89), kind=kLoop, calls=%fused_computation.38.clone.1 | loop fusion | bytes 4194308 | tf_op jit(solution)/shard_map/while/body/eval_jaxpr/dynamic_update_slice | solution.py:99
  142.6 0.5 copy-done.13
  143.3 0.6 constant_dynamic-slice_fusion.7
  143.9 2.8 constant_dynamic-slice_fusion.6
  146.7 11.9 %while.53 = (s32[]{:T(128)}, f32[512,1024]{0,1:T(8,128)S(1)}, f32[512,128]{1,0:T(8,128)}, f32[512,128]{1,0:T(8,128)S(1)}, bf16[512,128]{1,0:T(8,128)(2,1)S(1)}, ...) while((s32[]{:T(128)}, f32[512,1024]{0,1:T(8,128)S(1)}, ...), condition=%wide.region_3.3_spmd.clone, body=%wide.region_2.2_spmd.clone.sunk | while | flops 1354170368 | bytes 39578024 | solution.py:96
  147.0 0.7 fusion.79
  147.9 1.1 fusion.83
  149.1 1.6 fusion.80
  150.8 0.8 fusion.82
  151.5 0.5 fusion.81
  152.0 0.6 bitcast_add_fusion.2
  153.0 0.7 fusion.79
  153.9 1.1 fusion.83
  155.1 1.6 fusion.80
  156.7 0.8 fusion.82
  157.5 0.5 fusion.81
  158.0 0.6 bitcast_add_fusion.2
  158.6 1.9 copy.56
  160.5 3.2 %constant_dynamic-update-slice_fusion.2 = f32[1024,1024]{1,0:T(8,128)} fusion(f32[1024,1024]{1,0:T(8,128)} %get-tuple-element.913, f32[512,1024]{1,0:T(8,128)} %copy.56, s32[]{:T(128)S(6)} %select_n.89), kind=kLoop, calls=%fused_computation.38.clone.1 | loop fusion | bytes 4194308 | tf_op jit(solution)/shard_map/while/body/eval_jaxpr/dynamic_update_slice | solution.py:99
  163.8 0.7 copy-done.1
  164.6 1.7 broadcast_multiply_fusion.1
  166.3 5.1 %broadcast_multiply_fusion = f32[1024,1024]{1,0:T(8,128)} fusion(f32[1024,1024]{1,0:T(8,128)} %get-tuple-element.501), kind=kLoop, calls=%fused_computation.43 | loop fusion | flops 1048576 | bytes 8388608 | tf_op jit(solution)/shard_map/mul | solution.py:149
  171.4 11.8 %reduce-scatter.8.cloned.1.call-done = f32[128,128]{1,0:T(8,128)} async-done(((f32[512,128]{1,0:T(8,128)}), f32[128,128]{1,0:T(8,128)}) %reduce-scatter.8.cloned.1.call-update) | async-done | bytes 65552 | tf_op jit(solution)/shard_map/reduce_scatter | solution.py:152
  183.3 1.5 convert_element_type.33
  184.7 21.5 %reduce-scatter.6.cloned.1.call-done = f32[128,128]{1,0:T(8,128)} async-done(((f32[512,128]{1,0:T(8,128)}), f32[128,128]{1,0:T(8,128)}) %reduce-scatter.6.cloned.1.call-update) | async-done | bytes 65552 | tf_op jit(solution)/shard_map/reduce_scatter | solution.py:151
  206.2 1.5 convert_element_type.32
  207.7 90.4 %reduce-scatter.4.cloned.1.call-done = f32[128,1024]{1,0:T(8,128)} async-done(((f32[1024,1024]{1,0:T(8,128)}), f32[128,1024]{1,0:T(8,128)}) %reduce-scatter.4.cloned.1.call-update) | async-done | bytes 524304 | tf_op jit(solution)/shard_map/reduce_scatter | solution.py:149
  298.1 1.8 convert_element_type.31
  (118 shorter events, 3.0 us)
Async XLA Ops:
  7.2 56.3 %copy-start.15 = (s32[128]{0:T(128)S(1)}, s32[128]{0:T(128)}, u32[]{:S(2)}) copy-start(s32[128]{0:T(128)} %param.18) | copy-start | bytes 1540
  7.2 61.3 %copy-start.16 = (s32[128]{0:T(128)S(1)}, s32[128]{0:T(128)}, u32[]{:S(2)}) copy-start(s32[128]{0:T(128)} %param.19) | copy-start | bytes 1540
  7.2 101.3 %all-gather.7.cloned.1.call-start = ((), (), s32[]{:S(2)}) async-start(), calls=%async_computation.3 | async-start | bytes 2359296 | tf_op jit(solution)/shard_map/all_gather | solution.py:122
  7.9 110.2 %all-gather.9.cloned.1.call-start = ((), (), s32[]{:S(2)}) async-start(), calls=%async_computation.4 | async-start | bytes 2359296 | tf_op jit(solution)/shard_map/all_gather | solution.py:123
  8.7 174.6 %reduce-scatter.8.cloned.1.call-start = ((), (), s32[]{:S(2)}) async-start(), calls=%async_computation.7 | async-start | bytes 327680 | tf_op jit(solution)/shard_map/reduce_scatter | solution.py:152
  8.7 9.8 %collective-permute-start = (f32[8,128]{1,0:T(8,128)}, f32[8,128]{1,0:T(8,128)S(1)}, u32[]{:S(2)}, u32[]{:S(2)}) collective-permute-start(f32[8,128]{1,0:T(8,128)} %param.17), channel_id=1, source_target_pairs={{0,1},{1,0},{2,3},{3,2},{4,5},{5,4},{6,7},{7,6},{8,9},{9,8},{10,11... | collective-permute-start | bytes 12296 | tf_op jit(solution)/shard_map/ppermute | solution.py:11
  19.3 8.8 %collective-permute-start.1 = (f32[8,256]{1,0:T(8,128)S(1)}, f32[8,256]{1,0:T(8,128)S(1)}, u32[]{:S(2)}, u32[]{:S(2)}) collective-permute-start(f32[8,256]{1,0:T(8,128)S(1)} %maximum_select_fusion.2), channel_id=1, source_target_pairs={{0,2},{1,3},{2,0},{3,1},{4,6},{5,7},{6,4},{7,5},{8,10},{9,11},{10,... | collective-permute-start | bytes 24584 | tf_op jit(solution)/shard_map/ppermute | solution.py:11
  28.1 80.4 %collective-permute-start.2 = (f32[8,512]{1,0:T(8,128)S(1)}, f32[8,512]{1,0:T(8,128)S(1)}, u32[]{:S(2)}, u32[]{:S(2)}) collective-permute-start(f32[8,512]{1,0:T(8,128)S(1)} %maximum_select_fusion.1), channel_id=1, source_target_pairs={{0,4},{1,5},{2,6},{3,7},{4,0},{5,1},{6,2},{7,3},{8,12},{9,13},{10,... | collective-permute-start | bytes 49160 | tf_op jit(solution)/shard_map/ppermute | solution.py:11
  121.4 0.6 copy-start.13
  121.4 1.3 copy-start.6
  121.4 1.3 copy-start.8
  121.4 1.3 copy-start.11
  125.5 1.2 copy-start
  125.5 1.2 copy-start.5
  126.8 1.2 copy-start.4
  126.8 1.2 copy-start.10
  127.9 1.6 copy-start.2
  130.3 1.1 copy-start.3
  131.5 1.2 copy-start
  131.5 1.2 copy-start.5
  132.7 1.2 copy-start.4
  132.7 1.2 copy-start.10
  133.9 1.6 copy-start.2
  136.3 1.1 copy-start.3
  137.4 5.1 %copy-start.14 = (s32[1024]{0:T(1024)S(1)}, s32[1024]{0:T(1024)}, u32[]{:S(2)}) copy-start(s32[1024]{0:T(1024)} %copy-done.13) | copy-start | bytes 12292 | tf_op jit(solution)/shard_map/while
  139.3 3.2 %copy-start.7 = (f32[8,1024]{1,0:T(8,128)S(1)}, f32[8,1024]{1,0:T(8,128)}, u32[]{:S(2)}) copy-start(f32[8,1024]{1,0:T(8,128)} %copy-done.6) | copy-start | bytes 98308 | tf_op jit(solution)/shard_map/while
  139.3 3.2 %copy-start.9 = (f32[8,1024]{1,0:T(8,128)S(1)}, f32[8,1024]{1,0:T(8,128)}, u32[]{:S(2)}) copy-start(f32[8,1024]{1,0:T(8,128)} %copy-done.8) | copy-start | bytes 98308 | tf_op jit(solution)/shard_map/while
  139.3 3.2 %copy-start.12 = (s32[1024]{0:T(1024)S(1)}, s32[1024]{0:T(1024)}, u32[]{:S(2)}) copy-start(s32[1024]{0:T(1024)} %copy-done.11) | copy-start | bytes 12292 | tf_op jit(solution)/shard_map/while
  142.6 0.6 copy-start.13
  142.6 1.3 copy-start.6
  142.6 1.3 copy-start.8
  142.6 1.3 copy-start.11
  146.7 1.2 copy-start
  146.7 1.2 copy-start.5
  147.9 1.2 copy-start.4
  147.9 1.2 copy-start.10
  149.1 1.6 copy-start.2
  151.5 1.1 copy-start.3
  152.7 1.2 copy-start
  152.7 1.2 copy-start.5
  153.9 1.2 copy-start.4
  153.9 1.2 copy-start.10
  155.1 1.6 copy-start.2
  157.5 1.1 copy-start.3
  158.6 5.2 %copy-start.14 = (s32[1024]{0:T(1024)S(1)}, s32[1024]{0:T(1024)}, u32[]{:S(2)}) copy-start(s32[1024]{0:T(1024)} %copy-done.13) | copy-start | bytes 12292 | tf_op jit(solution)/shard_map/while
  160.5 3.3 %copy-start.7 = (f32[8,1024]{1,0:T(8,128)S(1)}, f32[8,1024]{1,0:T(8,128)}, u32[]{:S(2)}) copy-start(f32[8,1024]{1,0:T(8,128)} %copy-done.6) | copy-start | bytes 98308 | tf_op jit(solution)/shard_map/while
  160.5 3.3 %copy-start.9 = (f32[8,1024]{1,0:T(8,128)S(1)}, f32[8,1024]{1,0:T(8,128)}, u32[]{:S(2)}) copy-start(f32[8,1024]{1,0:T(8,128)} %copy-done.8) | copy-start | bytes 98308 | tf_op jit(solution)/shard_map/while
  160.5 3.3 %copy-start.12 = (s32[1024]{0:T(1024)S(1)}, s32[1024]{0:T(1024)}, u32[]{:S(2)}) copy-start(s32[1024]{0:T(1024)} %copy-done.11) | copy-start | bytes 12292 | tf_op jit(solution)/shard_map/while
  163.8 0.7 copy-start.1
  164.5 41.7 %reduce-scatter.6.cloned.1.call-start = ((), (), s32[]{:S(2)}) async-start(), calls=%async_computation.6 | async-start | bytes 327680 | tf_op jit(solution)/shard_map/reduce_scatter | solution.py:151
  166.3 131.8 %reduce-scatter.4.cloned.1.call-start = ((), (), s32[]{:S(2)}) async-start(), calls=%async_computation.5 | async-start | bytes 4718592 | tf_op jit(solution)/shard_map/reduce_scatter | solution.py:149
Sparse Core Ops, SparseCore 0:
  10.1 57.0 all-gather.6
  69.3 48.6 all-gather.8
  164.6 18.5 reduce-scatter.7
  186.1 20.0 reduce-scatter.5
  209.7 88.3 reduce-scatter.3
